TPU v7x, 32 devices: a whole 2x2x4 slice. The times are simulated.
32 devices in a mesh: row: 8 (over z, y), col: 2 (over core), depth: 2 (over x).
Axes of the slice: x: 2, y: 2, z: 4, core: 2. Of those that a mesh axis runs over, the one named last changes fastest.
Arguments:
- student_hidden: bfloat16 [2048, 768], P('row', ('depth', 'col')), may hold values from -16 to 16
- embedding: bfloat16 [50304, 768], P('col', ('depth', 'row')), as said below
- teacher_logits: bfloat16 [2048, 50304], P('row', ('col', 'depth')), may hold values from -24 to 124, as said below
Outputs:
- loss: float32 [2048], P('row')
- peak_logprob: float32 [2048], P('row')
Inputs may be any that keep to these rules, and one draw needn't show every extreme that they name: embedding entries lie within plus or minus 4 / sqrt(768). teacher_logits lie within -24 and 124; each token's logits carry an offset of 0 to 100.
All inputs are finite; a program needn't handle non-finite values.
Results may differ from a plain program's by a relative error of at most 0.0003.
Values may be sent and summed in bfloat16 or wider, within the bound.
A program may use at most 128 MiB of HBM per device.

v0:
```python
import jax
import jax.numpy as jnp
from jax import lax
from jax.sharding import PartitionSpec as P


def row_terms(student, teacher_values, student_peak, teacher_peak):
    weights = jnp.exp(teacher_values - teacher_peak[:, None])
    student_sum = jnp.sum(jnp.exp(student - student_peak[:, None]), axis=1)
    teacher_sum = jnp.sum(weights, axis=1)
    cross_sum = jnp.sum(weights * student, axis=1)
    return (student_sum, teacher_sum, cross_sum)


def on_device(student_hidden, embedding, teacher_logits):
    hidden_layer = lax.all_gather(student_hidden, "col", axis=1, tiled=True)
    token_count = hidden_layer.shape[0]
    hidden_full = lax.all_gather(hidden_layer, "depth", axis=1, tiled=True)
    row_count = lax.axis_size("row")
    depth_count = lax.axis_size("depth")
    narrow = embedding.shape[1]
    hidden_order = hidden_full.reshape(token_count, depth_count, row_count, narrow)
    hidden_order = hidden_order.transpose(0, 2, 1, 3).reshape(
        token_count, row_count * depth_count * narrow
    )
    vocab_rows = lax.all_to_all(embedding, "depth", split_axis=0, concat_axis=1, tiled=True)
    full_rows = lax.all_gather(vocab_rows, "row", axis=1, tiled=True)
    student = jnp.einsum("td,vd->tv", hidden_order, full_rows, preferred_element_type=jnp.float32)
    teacher_values = teacher_logits.astype(jnp.float32)
    student_top = jnp.max(student, axis=1)
    teacher_top = jnp.max(teacher_values, axis=1)
    student_peak, teacher_peak = lax.pmax((student_top, teacher_top), ("col", "depth"))
    local_student, local_teacher, local_cross = row_terms(
        student, teacher_values, student_peak, teacher_peak
    )
    student_sum, teacher_sum, cross_sum = lax.psum(
        (local_student, local_teacher, local_cross), ("col", "depth")
    )
    norm_log = jnp.log(student_sum)
    loss = student_peak + norm_log - cross_sum / teacher_sum
    return (loss, -norm_log)


def solution(mesh):
    in_specs = (P("row", ("depth", "col")), P("col", ("depth", "row")), P("row", ("col", "depth")))
    out_specs = (P("row"), P("row"))
    return jax.shard_map(
        on_device, mesh=mesh, in_specs=in_specs, out_specs=out_specs, check_vma=False
    )
```

profile of v0, /device:TPU:0, one launch (start us, length us, event | category | flops | bytes accessed | tf_op | source)
XLA Modules:
  0.0 464.3 jit_solution(10611060444776623536)
XLA Ops:
  7.2 0.0 copy-start
  7.2 0.0 all-gather.2.cloned.1.call-start
  7.2 3.9 all_to_all.14
  11.1 0.2 copy.8
  11.4 33.4 %all_to_all.19 = bf16[2,12576,48]{1,2,0:T(8,128)(2,1)} all-to-all(bf16[2,12576,48]{1,2,0:T(8,128)(2,1)S(1)} %copy.8), channel_id=1, replica_groups=mesh['row'=8,'col'=2,'depth'=2] {'depth'}, dimensions={0} | all-to-all | bytes 4829184 | tf_op jit(solution)/shard_map/all_to_all | solution.py:26
  44.8 0.0 all-gather.2.cloned.1.call-update
  44.8 0.0 copy-done
  44.8 1.9 all_gather.9
  46.8 7.6 %all_gather.10 = bf16[256,768]{0,1:T(8,128)(2,1)S(1)} all-gather(bf16[256,384]{0,1:T(8,128)(2,1)S(1)} %all_gather.9), channel_id=1, replica_groups=mesh['row'=8,'col'=2,'depth'=2] {'depth'}, dimensions={1}, use_global_device_ids=true | all-gather | bytes 589824 | tf_op jit(solution)/shard_map/all_gather | solution.py:18
  54.4 4.4 reduce_max.24
  58.8 360.2 %all-gather.2.cloned.1.call-done = bf16[12576,768]{0,1:T(8,128)(2,1)} async-done(((bf16[12576,96]{0,1:T(8,128)(2,1)}), bf16[12576,768]{0,1:T(8,128)(2,1)}) %all-gather.2.cloned.1.call-update) | async-done | bytes 19316752 | tf_op jit(solution)/shard_map/all_gather | solution.py:27
  419.0 14.5 %fusion.1 = (f32[256]{0:T(256)S(1)}, f32[256,12576]{0,1:T(8,128)}) fusion(bf16[256,768]{0,1:T(8,128)(2,1)S(1)} %bitcast.12, bf16[12576,768]{0,1:T(8,128)(2,1)} %all-gather.2.cloned.1.call-done), kind=kOutput, calls=%fused_computation.6 | convolution fusion | flops 4948303872 | bytes 32588800 | tf_op jit(solution)/shard_map/td,vd->tv/dot_general | solution.py:28
  433.5 7.4 %all-reduce.1 = (f32[256]{0:T(256)S(1)}, f32[256]{0:T(256)S(1)}) all-reduce(f32[256]{0:T(256)S(1)} %get-tuple-element.12, bf16[256]{0:T(256)(128)(2,1)S(1)} %reduce_max.24), channel_id=1, replica_groups=mesh['row'=8,'col'=2,'depth'=2] {'col','depth'}, use_global_device_ids=true, to_apply=%region_1.0 | all-reduce | flops 512 | bytes 3584 | tf_op jit(solution)/shard_map/pmax | solution.py:32
  440.9 8.9 %exponential_reduce_fusion = (f32[256]{0:T(256)S(1)}, f32[256]{0:T(256)S(1)}, f32[256]{0:T(256)S(1)}) fusion(f32[256,12576]{0,1:T(8,128)} %get-tuple-element.13, f32[256]{0:T(256)S(1)} %get-tuple-element.8, f32[256]{0:T(256)S(1)} %get-tuple-element.9, bf16[256,12576]{0,1:T(8,128)(2,1)} %param.5), kind=kLoop, calls=%fused_computation.3 | loop fusion | flops 22535424 | bytes 19321856 | tf_op jit(solution)/shard_map/reduce_sum | solution.py:9
  449.8 7.1 %all-reduce = (f32[256]{0:T(256)S(1)}, f32[256]{0:T(256)S(1)}, f32[256]{0:T(256)S(1)}) all-reduce(f32[256]{0:T(256)S(1)} %get-tuple-element.3, f32[256]{0:T(256)S(1)} %get-tuple-element.4, f32[256]{0:T(256)S(1)} %get-tuple-element.2), channel_id=1, replica_groups=mesh['row'=8,'col'=2,'depth'=2] {'col','depth'}, use_global_device_ids=true, to_apply=%region_7.0 | all-reduce | flops 768 | bytes 6144 | tf_op jit(solution)/shard_map/psum | solution.py:36
  456.9 0.6 log_negate_fusion
  (1 shorter events, 0.0 us)
Async XLA Ops:
  7.2 37.7 %copy-start = (bf16[256,192]{0,1:T(8,128)(2,1)S(1)}, bf16[256,192]{0,1:T(8,128)(2,1)}, u32[]{:S(2)}) copy-start(bf16[256,192]{0,1:T(8,128)(2,1)} %param.3) | copy-start | bytes 294916
  7.2 411.8 %all-gather.2.cloned.1.call-start = ((), (), s32[]{:S(2)}) async-start(), calls=%async_computation.1 | async-start | bytes 21897216 | tf_op jit(solution)/shard_map/all_gather | solution.py:27
Sparse Core Ops, SparseCore 0:
  44.9 374.0 all-gather.1
where the time goes:
time: 465 us; the launch traced here: 464 us
  waiting for transfers between devices  360 us (77%)
  blocking collectives  57.5 us (12%)
  matrix products  14.5 us (3%)
  between operations  14.1 us (3%)
  other arithmetic  13.8 us (3%)
    all_gather x1, waiting for transfers between devices, on_device(): full_rows = lax.all_gather(vocab_rows, 'row', axis=1, tiled=True)  360 us
    all_to_all x1, blocking collectives, on_device(): lax.all_to_all(embedding, 'depth', split_axis=0, concat_axis=1, tiled=True)  33.4 us
    dot_general x1, matrix products, on_device(): jnp.einsum('td,vd->tv', hidden_order, full_rows, preferred_element_type=j...  14.5 us
  transfers between devices with their start and end apart: 1, of which 1 were waited for; matrix products, arithmetic and copies ran while one was open for 1% of the time, Pallas kernels for 0%

commit v1 on v0

v1 whole, which is shorter than its diff:
```python
import functools

import jax
import jax.numpy as jnp
from jax import lax
from jax.experimental import pallas as pl
from jax.experimental.pallas import tpu as pltpu
from jax.sharding import PartitionSpec as P

MESH = pl.DeviceIdType.MESH
GROUP = 2
TILE = 640
LOW = -1e30


def place(rows, cols, depths):
    r, c, d = lax.axis_index("row"), lax.axis_index("col"), lax.axis_index("depth")
    return r, c, d, r // GROUP, lax.rem(r, GROUP)


def greet(targets):
    barrier = pltpu.get_barrier_semaphore()
    for row, col, depth in targets:
        pl.semaphore_signal(barrier, inc=1, device_id=(row, col, depth), device_id_type=MESH)
    return barrier


def group_peers(rows, cols, depths):
    r, c, d, q, j = place(rows, cols, depths)
    peers = []
    for dj in range(GROUP):
        for dc in range(cols):
            for dd in range(depths):
                if dj or dc or dd:
                    peers.append((q * GROUP + lax.rem(j + dj, GROUP), lax.rem(c + dc, cols), lax.rem(d + dd, depths), dj))
    return peers


def gather_kernel(
    rows, cols, depths, pieces_ref, teacher_ref, hidden_ref, full_ref, other_ref, hid_ref,
    own_sem, first_send, first_recv, right_send, left_send, line_recv, teach_send, teach_recv, hid_send, hid_recv,
):
    r, c, d, q, j = place(rows, cols, depths)
    steps = rows // GROUP
    count = depths * GROUP
    me = d * GROUP + j
    peers = group_peers(rows, cols, depths)

    def slot(block, piece):
        return (piece // GROUP) * rows + block * GROUP + lax.rem(piece, GROUP)

    barrier = greet([(a, b, e) for a, b, e, _ in peers])

    @pl.when(q + 1 < steps)
    def _():
        pl.semaphore_signal(barrier, inc=1, device_id=(r + GROUP, c, d), device_id_type=MESH)

    @pl.when(q > 0)
    def _():
        pl.semaphore_signal(barrier, inc=1, device_id=(r - GROUP, c, d), device_id_type=MESH)

    neighbours = (q + 1 < steps).astype(jnp.int32) + (q > 0).astype(jnp.int32)
    pl.semaphore_wait(barrier, len(peers) + neighbours)

    def first(off):
        target = lax.rem(me + off, count)
        return pltpu.make_async_remote_copy(
            src_ref=pieces_ref.at[target], dst_ref=full_ref.at[slot(q, me)],
            send_sem=first_send.at[off], recv_sem=first_recv.at[off],
            device_id=(q * GROUP + lax.rem(target, GROUP), c, target // GROUP), device_id_type=MESH,
        )

    def along(block, off, right, src=None):
        piece = lax.rem(me + count - off, count)
        at = slot(block, piece)
        sems = right_send if right else left_send
        return pltpu.make_async_remote_copy(
            src_ref=full_ref.at[at] if src is None else src, dst_ref=full_ref.at[at],
            send_sem=sems.at[block, off], recv_sem=line_recv.at[block, off],
            device_id=(r + GROUP if right else r - GROUP, c, d), device_id_type=MESH,
        )

    def both(block, off, src=None):
        @pl.when(q + 1 < steps)
        def _():
            along(block, off, True, src).start()

        @pl.when(q > 0)
        def _():
            along(block, off, False, src).start()

    both(q, 0, pieces_ref.at[me])
    firsts = [first(off) for off in range(1, count)]
    for copy in firsts:
        copy.start()
    hids = []
    for n, (a, b, e, dj) in enumerate(peers):
        hids.append(pltpu.make_async_remote_copy(
            src_ref=hidden_ref, dst_ref=hid_ref.at[dj, d * cols + c], send_sem=hid_send.at[n], recv_sem=hid_recv.at[n],
            device_id=(a, b, e), device_id_type=MESH,
        ))
        hids[-1].start()
    pj = lax.rem(j + 1, GROUP)
    teach = pltpu.make_async_remote_copy(
        src_ref=teacher_ref.at[pj], dst_ref=other_ref, send_sem=teach_send, recv_sem=teach_recv,
        device_id=(q * GROUP + pj, c, d), device_id_type=MESH,
    )
    teach.start()
    own = pltpu.make_async_copy(pieces_ref.at[me], full_ref.at[slot(q, me)], own_sem.at[0])
    own.start()
    own_hid = pltpu.make_async_copy(hidden_ref, hid_ref.at[0, d * cols + c], own_sem.at[1])
    own_hid.start()

    for off in range(1, count):
        firsts[off - 1].wait_recv()
        both(q, off)

    def step(k, _):
        for off in range(count):
            @pl.when(q - k >= 0)
            def _():
                along(q - k, off, True).wait_recv()

                @pl.when(q + 1 < steps)
                def _():
                    along(q - k, off, True).start()

            @pl.when(q + k < steps)
            def _():
                along(q + k, off, False).wait_recv()

                @pl.when(q > 0)
                def _():
                    along(q + k, off, False).start()

        return 0

    lax.fori_loop(1, steps, step, 0)

    def settle(block, _):
        for off in range(count):
            @pl.when((block <= q) & (q + 1 < steps))
            def _():
                along(block, off, True).wait_send()

            @pl.when((block >= q) & (q > 0))
            def _():
                along(block, off, False).wait_send()

        return 0

    lax.fori_loop(0, steps, settle, 0)
    for copy in firsts:
        copy.wait_send()
    for copy in hids:
        copy.wait()
    teach.wait()
    own.wait()
    own_hid.wait()


def gather(rows, cols, depths, pieces, teacher, hidden):
    count, narrow, width = pieces.shape
    steps = rows // GROUP
    features, tokens = hidden.shape
    peers = GROUP * cols * depths - 1
    dma = pltpu.SemaphoreType.DMA
    any_space = pl.BlockSpec(memory_space=pl.ANY)
    return pl.pallas_call(
        functools.partial(gather_kernel, rows, cols, depths),
        out_shape=(
            jax.ShapeDtypeStruct((depths * rows, narrow, width), pieces.dtype),
            jax.ShapeDtypeStruct((width, tokens), teacher.dtype),
            jax.ShapeDtypeStruct((GROUP, depths * cols, features, tokens), hidden.dtype),
        ),
        in_specs=[any_space] * 3,
        out_specs=[any_space] * 3,
        scratch_shapes=[
            dma((2,)), dma((count,)), dma((count,)), dma((steps, count)), dma((steps, count)), dma((steps, count)),
            dma, dma, dma((peers,)), dma((peers,)),
        ],
        compiler_params=pltpu.CompilerParams(collective_id=0, has_side_effects=True),
        name="gather",
    )(pieces, teacher, hidden)


def add_terms(full_ref, teacher_refs, hid_ref, acc, start, size):
    rows = full_ref[:, :, pl.ds(start, size)].reshape(-1, size)
    for n, teacher_ref in enumerate(teacher_refs):
        hidden = hid_ref[n].reshape(rows.shape[0], -1)
        tokens = hidden.shape[1]
        student = lax.dot_general(rows, hidden, (((0,), (0,)), ((), ())), preferred_element_type=jnp.float32)
        student = student.reshape(size // 8, 8, tokens)
        teacher = teacher_ref[pl.ds(start, size), :].astype(jnp.float32).reshape(size // 8, 8, tokens)
        top = jnp.maximum(acc[n, 0], jnp.max(student, axis=0))
        acc[n, 1] = acc[n, 1] * jnp.exp(acc[n, 0] - top) + jnp.sum(jnp.exp(student - top[None]), axis=0)
        acc[n, 0] = top
        teacher_top = jnp.maximum(acc[n, 2], jnp.max(teacher, axis=0))
        fade = jnp.exp(acc[n, 2] - teacher_top)
        weights = jnp.exp(teacher - teacher_top[None])
        acc[n, 3] = acc[n, 3] * fade + jnp.sum(weights, axis=0)
        acc[n, 4] = acc[n, 4] * fade + jnp.sum(weights * student, axis=0)
        acc[n, 2] = teacher_top


def all_terms(full_ref, teacher_refs, hid_ref, out_ref, acc):
    width = full_ref.shape[2]
    for n in range(GROUP):
        for k in range(5):
            acc[n, k] = jnp.full(acc.shape[2:], LOW if k in (0, 2) else 0.0, jnp.float32)

    def tile(i, _):
        add_terms(full_ref, teacher_refs, hid_ref, acc, pl.multiple_of(i * TILE, TILE), TILE)
        return 0

    lax.fori_loop(0, width // TILE, tile, 0)
    if width % TILE:
        add_terms(full_ref, teacher_refs, hid_ref, acc, width - width % TILE, width % TILE)
    for n in range(GROUP):
        values = merge([acc[n, k] for k in range(5)])
        out_ref[n] = jnp.concatenate(values + [values[0]] * 3, axis=0)


def terms_kernel(j_ref, full_ref, own_ref, other_ref, hid_ref, out_ref, acc):
    all_terms(full_ref, (own_ref.at[0], other_ref), hid_ref, out_ref, acc)


def merge(parts):
    top, total, teacher_top, teacher_total, cross = parts
    peak = jnp.max(top, axis=0, keepdims=True)
    teacher_peak = jnp.max(teacher_top, axis=0, keepdims=True)
    scale = jnp.exp(teacher_top - teacher_peak)
    return [
        peak,
        jnp.sum(total * jnp.exp(top - peak), axis=0, keepdims=True),
        teacher_peak,
        jnp.sum(teacher_total * scale, axis=0, keepdims=True),
        jnp.sum(cross * scale, axis=0, keepdims=True),
    ]


def terms(j, full, teacher, other, hid):
    tokens = other.shape[1]
    return pl.pallas_call(
        terms_kernel,
        out_shape=jax.ShapeDtypeStruct((GROUP, 8, tokens), jnp.float32),
        grid_spec=pltpu.PrefetchScalarGridSpec(
            num_scalar_prefetch=1,
            grid=(1,),
            in_specs=[
                pl.BlockSpec(full.shape, lambda i, j: (0, 0, 0)),
                pl.BlockSpec((1,) + other.shape, lambda i, j: (j[0], 0, 0)),
                pl.BlockSpec(other.shape, lambda i, j: (0, 0)),
                pl.BlockSpec(hid.shape, lambda i, j: (0, 0, 0, 0)),
            ],
            out_specs=pl.BlockSpec((GROUP, 8, tokens), lambda i, j: (0, 0, 0)),
            scratch_shapes=[pltpu.VMEM((GROUP, 5, 8, tokens), jnp.float32)],
        ),
        compiler_params=pltpu.CompilerParams(vmem_limit_bytes=60 * 2**20),
        name="terms",
    )(j, full, teacher, other, hid)


def combine_kernel(rows, cols, depths, stats_ref, loss_ref, peak_ref, held, send_sem, recv_sem):
    peers = group_peers(rows, cols, depths)
    barrier = greet([(a, b, e) for a, b, e, _ in peers])
    pl.semaphore_wait(barrier, len(peers))
    copies = []
    for n, (a, b, e, dj) in enumerate(peers):
        copies.append(pltpu.make_async_remote_copy(
            src_ref=stats_ref.at[dj], dst_ref=held.at[n], send_sem=send_sem.at[n], recv_sem=recv_sem.at[n],
            device_id=(a, b, e), device_id_type=MESH,
        ))
        copies[-1].start()
    for copy in copies:
        copy.wait()
    blocks = [stats_ref[0]] + [held[n] for n in range(len(peers))]
    parts = [jnp.concatenate([block[k : k + 1] for block in blocks], axis=0) for k in range(5)]
    peak, total, _, teacher_total, cross = merge(parts)
    norm_log = jnp.log(total)
    loss_ref[...] = peak + norm_log - cross / teacher_total
    peak_ref[...] = -norm_log


def combine(rows, cols, depths, stats):
    tokens = stats.shape[2]
    peers = GROUP * cols * depths - 1
    vmem = pl.BlockSpec(memory_space=pltpu.VMEM)
    return pl.pallas_call(
        functools.partial(combine_kernel, rows, cols, depths),
        out_shape=(jax.ShapeDtypeStruct((1, tokens), jnp.float32),) * 2,
        in_specs=[vmem],
        out_specs=(vmem, vmem),
        scratch_shapes=[
            pltpu.VMEM((peers, 8, tokens), jnp.float32),
            pltpu.SemaphoreType.DMA((peers,)),
            pltpu.SemaphoreType.DMA((peers,)),
        ],
        compiler_params=pltpu.CompilerParams(collective_id=1, has_side_effects=True),
        name="combine",
    )(stats)


def on_device(rows, cols, depths, student_hidden, embedding, teacher_logits):
    vocab, narrow = embedding.shape
    width = vocab // (depths * GROUP)
    pieces = embedding.T.reshape(narrow, depths * GROUP, width).transpose(1, 0, 2)
    teacher = teacher_logits.T.reshape(GROUP, width, -1)
    full, other, hid = gather(rows, cols, depths, pieces, teacher, student_hidden.T)
    j = lax.rem(lax.axis_index("row"), GROUP).astype(jnp.int32).reshape(1)
    loss, peak = combine(rows, cols, depths, terms(j, full, teacher, other, hid))
    return loss.reshape(-1), peak.reshape(-1)


def solution(mesh):
    sizes = [mesh.shape[name] for name in ("row", "col", "depth")]
    in_specs = (P("row", ("depth", "col")), P("col", ("depth", "row")), P("row", ("col", "depth")))
    out_specs = (P("row"), P("row"))
    return jax.shard_map(
        functools.partial(on_device, *sizes), mesh=mesh, in_specs=in_specs, out_specs=out_specs, check_vma=False
    )
```

time: 465 us -> 205 us (0.44)
  waiting for transfers between devices: 360 us -> 0 us
  Pallas kernels: 0 us -> 196 us
  blocking collectives: 57.5 us -> 0 us
  matrix products: 14.5 us -> 0 us
  other arithmetic: 13.8 us -> 0 us
  between operations: 14.1 us -> 0.66 us
  local copies, waits for them, and re-layouts: 4.17 us -> 8.97 us
    all_gather x1 -> x0, waiting for transfers between devices: 360 us -> none  [on_device(): full_rows = lax.all_gather(vocab_rows, 'row', axis=1, tiled=True)]
    pallas_call x0 -> x3, Pallas kernels: none -> 196 us  [the longest x1 167 us: gather(): pl.pallas_call(functools.partial(gather_kernel, rows, cols, depths), out_...]
    all_to_all x1 -> x0, blocking collectives: 33.4 us -> none  [on_device(): lax.all_to_all(embedding, 'depth', split_axis=0, concat_axis=1, tiled=True)]
    dot_general x1 -> x0, matrix products: 14.5 us -> none  [on_device(): jnp.einsum('td,vd->tv', hidden_order, full_rows, preferred_element_type=j...]
    all_gather x2 -> x0, blocking collectives: 9.55 us -> none  [the longest x1 7.61 us: on_device(): hidden_full = lax.all_gather(hidden_layer, 'depth', axis=1, tiled=True)]
    reduce_sum x1 -> x0, other arithmetic: 8.9 us -> none  [row_terms(): student_sum = jnp.sum(jnp.exp(student - student_peak[:, None]), axis=1)]
    pmax x1 -> x0, blocking collectives: 7.39 us -> none  [on_device(): lax.pmax((student_top, teacher_top), ('col', 'depth'))]
    psum x1 -> x0, blocking collectives: 7.12 us -> none  [on_device(): lax.psum((local_student, local_teacher, local_cross), ('col', 'depth'))]
  transfers between devices with their start and end apart: 1 -> 0, of which waited for: 1 -> 0; matrix products, arithmetic and copies ran while one was open for 1% -> 0% of each run, Pallas kernels for 0% -> 0%
where the time goes in v1:
time: 205 us
  Pallas kernels  196 us (96%)
  local copies, waits for them, and re-layouts  8.97 us (4%)
    pallas_call x1, Pallas kernels, gather(): pl.pallas_call(functools.partial(gather_kernel, rows, cols, depths), out_...  167 us
    pallas_call x1, Pallas kernels, terms(): pl.pallas_call(terms_kernel, out_shape=jax.ShapeDtypeStruct((GROUP, 8, to...  16.9 us
    pallas_call x1, Pallas kernels, combine(): pl.pallas_call(functools.partial(combine_kernel, rows, cols, depths), out...  11.9 us
    reshape x2, local copies, waits for them, and re-layouts, on_device(): embedding.T.reshape(narrow, depths * GROUP, width).transpose(1, 0, 2)  6.52 us

profile of v1, /device:TPU:0, one launch (start us, length us, event | category | flops | bytes accessed | tf_op | source)
XLA Modules:
  0.0 205.1 jit_solution(4574284698764129304)
XLA Ops:
  0.6 4.9 %reshape.20 = bf16[48,4,6288]{2,1,0:T(4,128)(2,1)S(1)} reshape(bf16[48,25152]{1,0:T(8,128)(2,1)} %bitcast.14) | data formatting | bytes 4829184 | tf_op jit(solution)/shard_map/reshape | solution.py:307
  5.5 1.7 copy.7
  7.2 166.8 %gather.1 = (bf16[16,48,6288]{2,1,0:T(8,128)(2,1)}, bf16[6288,256]{1,0:T(8,128)(2,1)}, bf16[2,4,192,256]{3,2,1,0:T(8,128)(2,1)}) custom-call(bf16[4,48,6288]{2,1,0:T(8,128)(2,1)} %bitcast.13, bf16[2,6288,256]{2,1,0:T(8,128)(2,1)} %bitcast.11, bf16[192,256]{1,0:T(8,128)(2,1)} %bitcast.15), custom_call_target="tpu_custom_call" | custom-call | tf_op jit(solution)/shard_map/gather/pallas_call | solution.py:169
  173.9 16.9 %terms.1.stats_ref = f32[2,8,256]{2,1,0:T(8,128)} custom-call(s32[1]{0:T(128)} %bitcast.j_ref, bf16[16,48,6288]{2,1,0:T(8,128)(2,1)} %get-tuple-element.7.full_ref, bf16[2,6288,256]{2,1,0:T(8,128)(2,1)} %bitcast.12, bf16[6288,256]{1,0:T(8,128)(2,1)} %get-tuple-element.8.other_ref, bf16[2,4,192,256]{3,2,1,0:T(8,128)(2,1)} %get-tuple-element.9.hid_ref), custom_call_target="tpu_custom_call" | custom-call | tf_op jit(solution)/shard_map/terms/pallas_call | solution.py:244
  190.8 11.9 %combine.1 = (f32[1,256]{1,0:T(1,128)}, f32[1,256]{1,0:T(1,128)}) custom-call(f32[2,8,256]{2,1,0:T(8,128)} %terms.1.stats_ref), custom_call_target="tpu_custom_call" | custom-call | tf_op jit(solution)/shard_map/combine/pallas_call | solution.py:289
  202.7 1.2 copy.10
  203.9 1.2 copy.11

commit v2 on v1

v2 whole, which is shorter than its diff:
```python
import functools

import jax
import jax.numpy as jnp
from jax import lax
from jax.experimental import pallas as pl
from jax.experimental.pallas import tpu as pltpu
from jax.sharding import PartitionSpec as P

MESH = pl.DeviceIdType.MESH
GROUP = 2
TILE = 640
CHUNK = 1280
SKIP = 2
LOW = -1e30


def place(rows, cols, depths):
    r, c, d = lax.axis_index("row"), lax.axis_index("col"), lax.axis_index("depth")
    return r, c, d, r // GROUP, lax.rem(r, GROUP)


def greet(targets):
    barrier = pltpu.get_barrier_semaphore()
    for row, col, depth in targets:
        pl.semaphore_signal(barrier, inc=1, device_id=(row, col, depth), device_id_type=MESH)
    return barrier


def group_peers(rows, cols, depths):
    r, c, d, q, j = place(rows, cols, depths)
    peers = []
    for dj in range(GROUP):
        for dc in range(cols):
            for dd in range(depths):
                if dj or dc or dd:
                    peers.append((q * GROUP + lax.rem(j + dj, GROUP), lax.rem(c + dc, cols), lax.rem(d + dd, depths), dj))
    return peers


def ends(rows, q):
    steps = rows // GROUP
    low, high = q == 0, q == steps - 1
    return low | high, (q == 1) | (q == steps - 2), jnp.where(q * 2 < steps, GROUP, -GROUP)


def as_count(flag):
    return flag.astype(jnp.int32)


def gather_kernel(
    rows, cols, depths, pieces_ref, teacher_ref, hidden_ref, full_ref, other_ref, extra_ref, hid_ref,
    own_sem, first_send, first_recv, right_send, left_send, line_recv, teach_send, teach_recv, extra_send, extra_recv,
    hid_send, hid_recv, far_send, far_recv,
):
    r, c, d, q, j = place(rows, cols, depths)
    steps = rows // GROUP
    count = depths * GROUP
    chunks = full_ref.shape[2] // CHUNK
    kept = chunks - SKIP
    me = d * GROUP + j
    peers = group_peers(rows, cols, depths)
    end, server, inward = ends(rows, q)

    def slot(block, piece):
        return (piece // GROUP) * rows + block * GROUP + lax.rem(piece, GROUP)

    def lanes(t):
        return pl.ds(pl.multiple_of(t * CHUNK, CHUNK), CHUNK)

    barrier = greet([(a, b, e) for a, b, e, _ in peers])

    @pl.when(q + 1 < steps)
    def _():
        pl.semaphore_signal(barrier, inc=1, device_id=(r + GROUP, c, d), device_id_type=MESH)

    @pl.when(q > 0)
    def _():
        pl.semaphore_signal(barrier, inc=1, device_id=(r - GROUP, c, d), device_id_type=MESH)

    pl.semaphore_wait(barrier, len(peers) + as_count(q + 1 < steps) + as_count(q > 0))

    def first(t, off):
        target = lax.rem(me + off, count)
        return pltpu.make_async_remote_copy(
            src_ref=pieces_ref.at[target, :, lanes(t)], dst_ref=full_ref.at[slot(q, me), :, lanes(t)],
            send_sem=first_send.at[t, off], recv_sem=first_recv.at[t, off],
            device_id=(q * GROUP + lax.rem(target, GROUP), c, target // GROUP), device_id_type=MESH,
        )

    def along(block, t, off, right, own=False):
        piece = lax.rem(me + count - off, count)
        at = full_ref.at[slot(block, piece), :, lanes(t)]
        sems = right_send if right else left_send
        return pltpu.make_async_remote_copy(
            src_ref=pieces_ref.at[me, :, lanes(t)] if own else at, dst_ref=at,
            send_sem=sems.at[block, t, off], recv_sem=line_recv.at[block, t, off],
            device_id=(r + GROUP if right else r - GROUP, c, d), device_id_type=MESH,
        )

    def to_right(t):
        return (q + 1 < steps) & ((t < kept) | (q + 2 < steps))

    def to_left(t):
        return (q > 0) & ((t < kept) | (q > 1))

    def both(t, off, own=False):
        @pl.when(to_right(t))
        def _():
            along(q, t, off, True, own).start()

        @pl.when(to_left(t))
        def _():
            along(q, t, off, False, own).start()

    def launch(t, _):
        for off in range(1, count):
            first(t, off).start()
        return 0

    both(0, 0, True)
    lax.fori_loop(0, chunks, launch, 0)
    hids = []
    for n, (a, b, e, dj) in enumerate(peers):
        hids.append(pltpu.make_async_remote_copy(
            src_ref=hidden_ref, dst_ref=hid_ref.at[dj, d * cols + c], send_sem=hid_send.at[n], recv_sem=hid_recv.at[n],
            device_id=(a, b, e), device_id_type=MESH,
        ))
        hids[-1].start()
    pj = lax.rem(j + 1, GROUP)
    cut = kept * CHUNK
    tail = pl.ds(cut, other_ref.shape[0] - cut)

    def teach(n, part):
        return pltpu.make_async_remote_copy(
            src_ref=teacher_ref.at[pj, part], dst_ref=other_ref.at[part], send_sem=teach_send.at[n], recv_sem=teach_recv.at[n],
            device_id=(q * GROUP + pj, c, d), device_id_type=MESH,
        )

    teaches = [teach(0, tail), teach(1, pl.ds(0, cut))]
    for copy in teaches:
        copy.start()

    def extra(n):
        return pltpu.make_async_remote_copy(
            src_ref=teacher_ref.at[j, tail] if n == 0 else other_ref.at[tail], dst_ref=extra_ref.at[n],
            send_sem=extra_send.at[n], recv_sem=extra_recv.at[n], device_id=(r + inward, c, d), device_id_type=MESH,
        )

    far = [pltpu.make_async_remote_copy(
        src_ref=hidden_ref, dst_ref=hid_ref.at[GROUP, d * cols + c], send_sem=far_send.at[0], recv_sem=far_recv.at[0],
        device_id=(r + inward, c, d), device_id_type=MESH,
    )]
    for n, (a, b, e, dj) in enumerate(peers):
        far.append(pltpu.make_async_remote_copy(
            src_ref=hid_ref.at[GROUP, d * cols + c], dst_ref=hid_ref.at[GROUP + dj, d * cols + c],
            send_sem=far_send.at[n + 1], recv_sem=far_recv.at[n + 1], device_id=(a, b, e), device_id_type=MESH,
        ))

    @pl.when(end)
    def _():
        far[0].start()

    own = pltpu.make_async_copy(pieces_ref.at[me], full_ref.at[slot(q, me)], own_sem.at[0])
    own.start()
    own_hid = pltpu.make_async_copy(hidden_ref, hid_ref.at[0, d * cols + c], own_sem.at[1])
    own_hid.start()

    def start_line(t, _):
        @pl.when(t > 0)
        def _():
            both(t, 0, True)

        for off in range(1, count):
            first(t, off).wait_recv()
            both(t, off)
        return 0

    lax.fori_loop(0, chunks, start_line, 0)

    @pl.when(end)
    def _():
        extra(0).start()
        teaches[0].wait_recv()
        extra(1).start()

    @pl.when(server)
    def _():
        far[0].wait_recv()
        for copy in far[1:]:
            copy.start()

    def step(k, _):
        def chunk(t, _):
            wanted = (t < kept) | ~end
            for off in range(count):
                @pl.when((q - k >= 0) & wanted)
                def _():
                    along(q - k, t, off, True).wait_recv()

                    @pl.when(to_right(t))
                    def _():
                        along(q - k, t, off, True).start()

                @pl.when((q + k < steps) & wanted)
                def _():
                    along(q + k, t, off, False).wait_recv()

                    @pl.when(to_left(t))
                    def _():
                        along(q + k, t, off, False).start()

            return 0

        return lax.fori_loop(0, chunks, chunk, 0)

    lax.fori_loop(1, steps, step, 0)

    def settle(block, _):
        def chunk(t, _):
            for off in range(count):
                @pl.when((block <= q) & to_right(t))
                def _():
                    along(block, t, off, True).wait_send()

                @pl.when((block >= q) & to_left(t))
                def _():
                    along(block, t, off, False).wait_send()

            return 0

        return lax.fori_loop(0, chunks, chunk, 0)

    lax.fori_loop(0, steps, settle, 0)

    def settle_first(t, _):
        for off in range(1, count):
            first(t, off).wait_send()
        return 0

    lax.fori_loop(0, chunks, settle_first, 0)
    for copy in hids:
        copy.wait()
    teaches[1].wait()
    teaches[0].wait_send()
    own.wait()
    own_hid.wait()

    @pl.when(end)
    def _():
        far[0].wait_send()
        extra(0).wait_send()
        extra(1).wait_send()

    @pl.when(~end)
    def _():
        teaches[0].wait_recv()

    @pl.when(server)
    def _():
        extra(0).wait_recv()
        extra(1).wait_recv()
        for copy in far[1:]:
            copy.wait()


def gather(rows, cols, depths, pieces, teacher, hidden):
    count, narrow, padded = pieces.shape
    width = teacher.shape[1]
    steps = rows // GROUP
    chunks = padded // CHUNK
    features, tokens = hidden.shape
    peers = GROUP * cols * depths - 1
    dma = pltpu.SemaphoreType.DMA
    any_space = pl.BlockSpec(memory_space=pl.ANY)
    line = (steps, chunks, count)
    return pl.pallas_call(
        functools.partial(gather_kernel, rows, cols, depths),
        out_shape=(
            jax.ShapeDtypeStruct((depths * rows, narrow, padded), pieces.dtype),
            jax.ShapeDtypeStruct((width, tokens), teacher.dtype),
            jax.ShapeDtypeStruct((GROUP, width - (chunks - SKIP) * CHUNK, tokens), teacher.dtype),
            jax.ShapeDtypeStruct((2 * GROUP, depths * cols, features, tokens), hidden.dtype),
        ),
        in_specs=[any_space] * 3,
        out_specs=[any_space] * 4,
        scratch_shapes=[
            dma((2,)), dma((chunks, count)), dma((chunks, count)), dma(line), dma(line), dma(line),
            dma((2,)), dma((2,)), dma((2,)), dma((2,)), dma((peers,)), dma((peers,)), dma((peers + 1,)), dma((peers + 1,)),
        ],
        compiler_params=pltpu.CompilerParams(collective_id=0, has_side_effects=True),
        name="gather",
    )(pieces, teacher, hidden)


def add_terms(full_ref, teacher_refs, hid_ref, acc, start, size, offset=0, sets=range(GROUP)):
    rows = full_ref[:, :, pl.ds(start, size)].reshape(-1, size)
    for n, teacher_ref in zip(sets, teacher_refs):
        hidden = hid_ref[n].reshape(rows.shape[0], -1)
        tokens = hidden.shape[1]
        student = lax.dot_general(rows, hidden, (((0,), (0,)), ((), ())), preferred_element_type=jnp.float32)
        student = student.reshape(size // 8, 8, tokens)
        teacher = teacher_ref[pl.ds(start - offset, size), :].astype(jnp.float32).reshape(size // 8, 8, tokens)
        top = jnp.maximum(acc[n, 0], jnp.max(student, axis=0))
        acc[n, 1] = acc[n, 1] * jnp.exp(acc[n, 0] - top) + jnp.sum(jnp.exp(student - top[None]), axis=0)
        acc[n, 0] = top
        teacher_top = jnp.maximum(acc[n, 2], jnp.max(teacher, axis=0))
        fade = jnp.exp(acc[n, 2] - teacher_top)
        weights = jnp.exp(teacher - teacher_top[None])
        acc[n, 3] = acc[n, 3] * fade + jnp.sum(weights, axis=0)
        acc[n, 4] = acc[n, 4] * fade + jnp.sum(weights * student, axis=0)
        acc[n, 2] = teacher_top


def terms_kernel(flags, full_ref, own_ref, other_ref, extra_ref, hid_ref, out_ref, acc):
    width = other_ref.shape[0]
    cut = width - extra_ref.shape[1]
    for n in range(2 * GROUP):
        for k in range(5):
            acc[n, k] = jnp.full(acc.shape[2:], LOW if k in (0, 2) else 0.0, jnp.float32)
    main = (own_ref.at[0], other_ref)
    extra = tuple(extra_ref.at[n] for n in range(GROUP))

    def tiles(begin, stop, refs, offset, sets):
        whole = (stop - begin) // TILE

        def tile(i, _):
            start = pl.multiple_of(begin + i * TILE, 128)
            add_terms(full_ref, refs, hid_ref, acc, start, TILE, offset, sets)
            return 0

        lax.fori_loop(0, whole, tile, 0)
        if (stop - begin) % TILE:
            add_terms(full_ref, refs, hid_ref, acc, begin + whole * TILE, (stop - begin) % TILE, offset, sets)

    tiles(0, cut, main, 0, range(GROUP))

    @pl.when(flags[1] == 0)
    def _():
        tiles(cut, width, main, 0, range(GROUP))

    @pl.when(flags[2] == 1)
    def _():
        tiles(cut, width, extra, cut, range(GROUP, 2 * GROUP))

    for n in range(2 * GROUP):
        values = merge([acc[n, k] for k in range(5)])
        out_ref[n] = jnp.concatenate(values + [values[0]] * 3, axis=0)


def merge(parts):
    top, total, teacher_top, teacher_total, cross = parts
    peak = jnp.max(top, axis=0, keepdims=True)
    teacher_peak = jnp.max(teacher_top, axis=0, keepdims=True)
    scale = jnp.exp(teacher_top - teacher_peak)
    return [
        peak,
        jnp.sum(total * jnp.exp(top - peak), axis=0, keepdims=True),
        teacher_peak,
        jnp.sum(teacher_total * scale, axis=0, keepdims=True),
        jnp.sum(cross * scale, axis=0, keepdims=True),
    ]


def terms(flags, full, teacher, other, extra, hid):
    tokens = other.shape[1]
    return pl.pallas_call(
        terms_kernel,
        out_shape=jax.ShapeDtypeStruct((2 * GROUP, 8, tokens), jnp.float32),
        grid_spec=pltpu.PrefetchScalarGridSpec(
            num_scalar_prefetch=1,
            grid=(1,),
            in_specs=[
                pl.BlockSpec(full.shape, lambda i, f: (0, 0, 0)),
                pl.BlockSpec((1,) + other.shape, lambda i, f: (f[0], 0, 0)),
                pl.BlockSpec(other.shape, lambda i, f: (0, 0)),
                pl.BlockSpec(extra.shape, lambda i, f: (0, 0, 0)),
                pl.BlockSpec(hid.shape, lambda i, f: (0, 0, 0, 0)),
            ],
            out_specs=pl.BlockSpec((2 * GROUP, 8, tokens), lambda i, f: (0, 0, 0)),
            scratch_shapes=[pltpu.VMEM((2 * GROUP, 5, 8, tokens), jnp.float32)],
        ),
        compiler_params=pltpu.CompilerParams(vmem_limit_bytes=60 * 2**20),
        name="terms",
    )(flags, full, teacher, other, extra, hid)


def combine_kernel(rows, cols, depths, stats_ref, loss_ref, peak_ref, held, send_sem, recv_sem):
    r, c, d, q, j = place(rows, cols, depths)
    end, server, inward = ends(rows, q)
    peers = group_peers(rows, cols, depths)
    near = len(peers)
    group = [(r, c, d, 0)] + peers
    barrier = greet([(a, b, e) for a, b, e, _ in peers])

    @pl.when(end)
    def _():
        greet([(a + inward, b, e) for a, b, e, _ in group])

    @pl.when(server)
    def _():
        greet([(a - inward, b, e) for a, b, e, _ in group])

    pl.semaphore_wait(barrier, near + as_count(end | server) * len(group))

    def send(n, a, b, e, source):
        return pltpu.make_async_remote_copy(
            src_ref=stats_ref.at[source], dst_ref=held.at[n], send_sem=send_sem.at[n], recv_sem=recv_sem.at[n],
            device_id=(a, b, e), device_id_type=MESH,
        )

    copies = [send(n, a, b, e, dj) for n, (a, b, e, dj) in enumerate(peers)]
    far = [send(near + n, a - inward, b, e, GROUP + dj) for n, (a, b, e, dj) in enumerate(group)]

    @pl.when(server)
    def _():
        for copy in far:
            copy.start()

    for copy in copies:
        copy.start()

    @pl.when(~end)
    def _():
        for n in range(len(group)):
            for k in range(5):
                held[near + n, k] = jnp.full(held.shape[2:], LOW if k in (0, 2) else 0.0, jnp.float32)

    for copy in copies:
        copy.wait()

    @pl.when(server)
    def _():
        for copy in far:
            copy.wait_send()

    @pl.when(end)
    def _():
        for copy in far:
            copy.wait_recv()

    blocks = [stats_ref[0]] + [held[n] for n in range(near + len(group))]
    parts = [jnp.concatenate([block[k : k + 1] for block in blocks], axis=0) for k in range(5)]
    peak, total, _, teacher_total, cross = merge(parts)
    norm_log = jnp.log(total)
    loss_ref[...] = peak + norm_log - cross / teacher_total
    peak_ref[...] = -norm_log


def combine(rows, cols, depths, stats):
    tokens = stats.shape[2]
    slots = 2 * GROUP * cols * depths - 1
    vmem = pl.BlockSpec(memory_space=pltpu.VMEM)
    return pl.pallas_call(
        functools.partial(combine_kernel, rows, cols, depths),
        out_shape=(jax.ShapeDtypeStruct((1, tokens), jnp.float32),) * 2,
        in_specs=[vmem],
        out_specs=(vmem, vmem),
        scratch_shapes=[
            pltpu.VMEM((slots, 8, tokens), jnp.float32),
            pltpu.SemaphoreType.DMA((slots,)),
            pltpu.SemaphoreType.DMA((slots,)),
        ],
        compiler_params=pltpu.CompilerParams(collective_id=1, has_side_effects=True),
        name="combine",
    )(stats)


def on_device(rows, cols, depths, student_hidden, embedding, teacher_logits):
    vocab, narrow = embedding.shape
    width = vocab // (depths * GROUP)
    pieces = embedding.T.reshape(narrow, depths * GROUP, width).transpose(1, 0, 2)
    pieces = jnp.pad(pieces, ((0, 0), (0, 0), (0, -width % CHUNK)))
    teacher = teacher_logits.T.reshape(GROUP, width, -1)
    full, other, extra, hid = gather(rows, cols, depths, pieces, teacher, student_hidden.T)
    row = lax.axis_index("row")
    end, server, _ = ends(rows, row // GROUP)
    flags = jnp.stack([lax.rem(row, GROUP), as_count(end), as_count(server)]).astype(jnp.int32)
    loss, peak = combine(rows, cols, depths, terms(flags, full, teacher, other, extra, hid))
    return loss.reshape(-1), peak.reshape(-1)


def solution(mesh):
    sizes = [mesh.shape[name] for name in ("row", "col", "depth")]
    in_specs = (P("row", ("depth", "col")), P("col", ("depth", "row")), P("row", ("col", "depth")))
    out_specs = (P("row"), P("row"))
    return jax.shard_map(
        functools.partial(on_device, *sizes), mesh=mesh, in_specs=in_specs, out_specs=out_specs, check_vma=False
    )
```

time: 205 us -> 161 us (0.79)
  Pallas kernels: 196 us -> 151 us
    pallas_call x1, Pallas kernels: 167 us -> 116 us  [gather(): pl.pallas_call(functools.partial(gather_kernel, rows, cols, depths), out_...]
    pallas_call x1, Pallas kernels: 11.9 us -> 20.1 us  [combine(): pl.pallas_call(functools.partial(combine_kernel, rows, cols, depths), out...]
    pallas_call x1, Pallas kernels: 16.9 us -> 14.5 us  [terms(): pl.pallas_call(terms_kernel, out_shape=jax.ShapeDtypeStruct((2 * GROUP, 8...]
where the time goes in v2:
time: 161 us
  Pallas kernels  151 us (94%)
  local copies, waits for them, and re-layouts  9.1 us (6%)
    pallas_call x1, Pallas kernels, gather(): pl.pallas_call(functools.partial(gather_kernel, rows, cols, depths), out_...  116 us
    pallas_call x1, Pallas kernels, combine(): pl.pallas_call(functools.partial(combine_kernel, rows, cols, depths), out...  20.1 us
    pallas_call x1, Pallas kernels, terms(): pl.pallas_call(terms_kernel, out_shape=jax.ShapeDtypeStruct((2 * GROUP, 8...  14.5 us
    reshape x2, local copies, waits for them, and re-layouts, on_device(): embedding.T.reshape(narrow, depths * GROUP, width).transpose(1, 0, 2)  5.09 us

profile of v2, /device:TPU:0, one launch (start us, length us, event | category | flops | bytes accessed | tf_op | source)
XLA Modules:
  0.0 161.1 jit_solution(9441544678656728273)
XLA Ops:
  0.7 0.6 pad_add_fusion.flags
  1.3 4.8 %reshape.16 = bf16[48,4,6288]{2,1,0:T(4,128)(2,1)S(1)} reshape(bf16[48,25152]{1,0:T(8,128)(2,1)} %bitcast.16) | data formatting | bytes 4829184 | tf_op jit(solution)/shard_map/reshape | solution.py:472
  6.1 0.2 copy.7
  6.4 1.6 pad.4.pieces_ref
  7.9 116.1 %gather.1 = (bf16[16,48,6400]{2,1,0:T(8,128)(2,1)}, bf16[6288,256]{1,0:T(8,128)(2,1)}, bf16[2,2448,256]{2,1,0:T(8,128)(2,1)}, bf16[4,4,192,256]{3,2,1,0:T(8,128)(2,1)}) custom-call(bf16[4,48,6400]{2,1,0:T(8,128)(2,1)} %pad.4.pieces_ref, bf16[2,6288,256]{2,1,0:T(8,128)(2,1)} %bitcast.13, bf16[192,256]{1,0:T(8,128)(2,1)} %bitcast.17), custom_call_target="tpu_custom_call" | custom-call | tf_op jit(solution)/shard_map/gather/pallas_call | solution.py:277
  124.0 14.5 %terms.1.stats_ref = f32[4,8,256]{2,1,0:T(8,128)} custom-call(s32[3]{0:T(128)} %pad_add_fusion.flags, bf16[16,48,6400]{2,1,0:T(8,128)(2,1)} %get-tuple-element.8.full_ref, bf16[2,6288,256]{2,1,0:T(8,128)(2,1)} %bitcast.14, bf16[6288,256]{1,0:T(8,128)(2,1)} %get-tuple-element.9.other_ref, bf16[2,2448,256]{2,1,0:T(8,128)(2,1)} %get-tuple-element.10.extra_ref, ...), custom_call_target="tpu_custom_call" | custom-call | tf_op jit(solution)/shard_map/terms/pallas_call | solution.py:367
  138.5 20.1 %combine.1 = (f32[1,256]{1,0:T(1,128)}, f32[1,256]{1,0:T(1,128)}) custom-call(f32[4,8,256]{2,1,0:T(8,128)} %terms.1.stats_ref), custom_call_target="tpu_custom_call" | custom-call | tf_op jit(solution)/shard_map/combine/pallas_call | solution.py:454
  158.7 1.2 copy.10
  159.9 1.2 copy.11

commit v3 on v2

--- a/solution.py
+++ b/solution.py
@@ -10,8 +10,8 @@
 MESH = pl.DeviceIdType.MESH
 GROUP = 2
 TILE = 640
-CHUNK = 1280
-SKIP = 2
+CHUNK = 640
+SKIP = 3
 LOW = -1e30
 
 
@@ -50,7 +50,7 @@
 
 def gather_kernel(
     rows, cols, depths, pieces_ref, teacher_ref, hidden_ref, full_ref, other_ref, extra_ref, hid_ref,
-    own_sem, first_send, first_recv, right_send, left_send, line_recv, teach_send, teach_recv, extra_send, extra_recv,
+    own_sem, first_send, first_recv, line_send, line_recv, teach_send, teach_recv, extra_send, extra_recv,
     hid_send, hid_recv, far_send, far_recv,
 ):
     r, c, d, q, j = place(rows, cols, depths)
@@ -91,10 +91,9 @@
     def along(block, t, off, right, own=False):
         piece = lax.rem(me + count - off, count)
         at = full_ref.at[slot(block, piece), :, lanes(t)]
-        sems = right_send if right else left_send
         return pltpu.make_async_remote_copy(
             src_ref=pieces_ref.at[me, :, lanes(t)] if own else at, dst_ref=at,
-            send_sem=sems.at[block, t, off], recv_sem=line_recv.at[block, t, off],
+            send_sem=line_send.at[block if right else block + 1, t, off], recv_sem=line_recv.at[block, t, off],
             device_id=(r + GROUP if right else r - GROUP, c, d), device_id_type=MESH,
         )
 
@@ -285,7 +284,7 @@
         in_specs=[any_space] * 3,
         out_specs=[any_space] * 4,
         scratch_shapes=[
-            dma((2,)), dma((chunks, count)), dma((chunks, count)), dma(line), dma(line), dma(line),
+            dma((2,)), dma((chunks, count)), dma((chunks, count)), dma((steps + 1, chunks, count)), dma(line),
             dma((2,)), dma((2,)), dma((2,)), dma((2,)), dma((peers,)), dma((peers,)), dma((peers + 1,)), dma((peers + 1,)),
         ],
         compiler_params=pltpu.CompilerParams(collective_id=0, has_side_effects=True),

time: 161 us -> 162 us (level)
    pallas_call x1, Pallas kernels: 20.1 us -> 11.5 us  [combine(): pl.pallas_call(functools.partial(combine_kernel, rows, cols, depths), out...]
    pallas_call x1, Pallas kernels: 116 us -> 124 us  [gather(): pl.pallas_call(functools.partial(gather_kernel, rows, cols, depths), out_...]
where the time goes in v3:
time: 162 us; the launch traced here: 161 us
  Pallas kernels  151 us (93%)
  local copies, waits for them, and re-layouts  9.13 us (6%)
    pallas_call x1, Pallas kernels, gather(): pl.pallas_call(functools.partial(gather_kernel, rows, cols, depths), out_...  124 us
    pallas_call x1, Pallas kernels, terms(): pl.pallas_call(terms_kernel, out_shape=jax.ShapeDtypeStruct((2 * GROUP, 8...  15.4 us
    pallas_call x1, Pallas kernels, combine(): pl.pallas_call(functools.partial(combine_kernel, rows, cols, depths), out...  11.5 us
    reshape x2, local copies, waits for them, and re-layouts, on_device(): embedding.T.reshape(narrow, depths * GROUP, width).transpose(1, 0, 2)  5.09 us

profile of v3, /device:TPU:0, one launch (start us, length us, event | category | flops | bytes accessed | tf_op | source)
XLA Modules:
  0.0 161.4 jit_solution(4241459061522612896)
XLA Ops:
  0.7 0.7 pad_add_fusion.flags
  1.3 4.8 %reshape.16 = bf16[48,4,6288]{2,1,0:T(4,128)(2,1)S(1)} reshape(bf16[48,25152]{1,0:T(8,128)(2,1)} %bitcast.16) | data formatting | bytes 4829184 | tf_op jit(solution)/shard_map/reshape | solution.py:471
  6.2 0.2 copy.7
  6.4 1.6 pad.4.pieces_ref
  8.0 124.1 %gather.1 = (bf16[16,48,6400]{2,1,0:T(8,128)(2,1)}, bf16[6288,256]{1,0:T(8,128)(2,1)}, bf16[2,1808,256]{2,1,0:T(8,128)(2,1)}, bf16[4,4,192,256]{3,2,1,0:T(8,128)(2,1)}) custom-call(bf16[4,48,6400]{2,1,0:T(8,128)(2,1)} %pad.4.pieces_ref, bf16[2,6288,256]{2,1,0:T(8,128)(2,1)} %bitcast.13, bf16[192,256]{1,0:T(8,128)(2,1)} %bitcast.17), custom_call_target="tpu_custom_call" | custom-call | tf_op jit(solution)/shard_map/gather/pallas_call | solution.py:276
  132.1 15.4 %terms.1.stats_ref = f32[4,8,256]{2,1,0:T(8,128)} custom-call(s32[3]{0:T(128)} %pad_add_fusion.flags, bf16[16,48,6400]{2,1,0:T(8,128)(2,1)} %get-tuple-element.8.full_ref, bf16[2,6288,256]{2,1,0:T(8,128)(2,1)} %bitcast.14, bf16[6288,256]{1,0:T(8,128)(2,1)} %get-tuple-element.9.other_ref, bf16[2,1808,256]{2,1,0:T(8,128)(2,1)} %get-tuple-element.10.extra_ref, ...), custom_call_target="tpu_custom_call" | custom-call | tf_op jit(solution)/shard_map/terms/pallas_call | solution.py:366
  147.5 11.5 %combine.1 = (f32[1,256]{1,0:T(1,128)}, f32[1,256]{1,0:T(1,128)}) custom-call(f32[4,8,256]{2,1,0:T(8,128)} %terms.1.stats_ref), custom_call_target="tpu_custom_call" | custom-call | tf_op jit(solution)/shard_map/combine/pallas_call | solution.py:453
  159.0 1.2 copy.10
  160.2 1.2 copy.11
